TPU v7x, 256 devices: a whole 4x4x8 slice. The times are simulated.
256 devices in a mesh: kf: 64 (over z, y, core), kc: 4 (over x).
Axes of the slice: x: 4, y: 4, z: 8, core: 2. Of those that a mesh axis runs over, the one named last changes fastest.
Arguments:
- kernel_coarse: bfloat16 [2048, 2048], P('kf'), may hold values from -6 to 6
- coefficients: bfloat16 [1024, 256], P(('kf', 'kc')), may hold values from -1.5 to 1.5
- nearest: int32 [1024], replicated, may hold values from 0 to 127
Outputs:
- kernel_fine: bfloat16 [16384, 16384], P('kf', 'kc')
All inputs are finite; a program needn't handle non-finite values.
Results may differ from a plain program's by a relative error of at most 0.0049.
Values may be sent and summed in bfloat16 or wider, within the bound.
No kernel may reach another device: no remote copies, remote signals or barrier semaphores. Data moves between devices by JAX's collectives and lax.ppermute only.
A program may use at most 64 MiB of HBM per device.

v0:
```python
import jax
import jax.numpy as jnp
from jax import lax
from jax.experimental import pallas as pl
from jax.experimental.pallas import tpu as pltpu
from jax.sharding import Mesh
from jax.sharding import PartitionSpec as P


KF = ("kf_0", "kf_1", "kf_2")
ZY = ("kf_0", "kf_1")
KF_KC = ("kf_0", "kf_1", "kf_2", "kc")
LANES = 128
PAIRS = 16
POINTS = 4
PEERS = 32
FINE = 1024
BF16 = jnp.bfloat16
F32 = jnp.float32
VMEM = pl.BlockSpec(memory_space=pltpu.VMEM)
SMEM = pl.BlockSpec(memory_space=pltpu.SMEM)
ANY = pl.BlockSpec(memory_space=pl.ANY)


def iota(shape, dim):
    return lax.broadcasted_iota(jnp.int32, shape, dim)


def dot_t(a, b):
    return lax.dot_general(a, b, (((1,), (1,)), ((), ())), preferred_element_type=F32)


def turn_rows(rows, copies):
    for b in range(16):
        block = rows[:32, b * LANES : (b + 1) * LANES].astype(F32)
        for s in range(8):
            turned = pltpu.roll(block, s * PAIRS, 1) if s else block
            copies[s * 16 + b] = turned.astype(BF16)


def halves_stacked(coef):
    return jnp.concatenate([coef[:, :LANES], coef[:, LANES:]], axis=0)


def own_kernel(fetched, copies, near, slots, coef):
    c = fetched[32:33, :FINE].astype(jnp.int32)
    near[...] = c
    slots[...] = ((iota((1, FINE), 1) % POINTS - c) & 7) * 16 + (c >> 3)
    coef[...] = halves_stacked(fetched[40:44, : 2 * LANES]).astype(BF16)
    turn_rows(fetched, copies)


def index_copy(near, scalars, sem):
    return pltpu.make_async_copy(near, scalars, sem.at[0])


def pack_kernel(slots, own_copies, other, coef, out, other_copies, scalars, sem):
    fetch = index_copy(slots, scalars, sem)
    fetch.start()
    kc = lax.axis_index("kc")
    core = lax.axis_index("kf_2")
    turn_rows(other, other_copies)
    copies = (own_copies, other_copies)
    fetch.wait()
    group = iota((PAIRS, LANES), 1) // PAIRS
    base = 16 * core + 4 * kc

    def body(d, carry):
        tiles = [None, None]
        for j in range(POINTS):
            slot = scalars[0, 32 * d + base + j]
            for lo in range(2):
                for n in range(2):
                    piece = copies[n][slot ^ (64 * lo), lo * PAIRS : (lo + 1) * PAIRS, :]
                    tiles[n] = piece if tiles[n] is None else jnp.where(group == lo * POINTS + j, piece, tiles[n])
        out[d, pl.ds(pl.multiple_of(core * PAIRS, PAIRS), PAIRS), :] = tiles[0]
        out[d, pl.ds(pl.multiple_of((1 - core) * PAIRS, PAIRS), PAIRS), :] = tiles[1]
        out[d, 2 * PAIRS :, :] = coef[...]
        return carry

    lax.fori_loop(0, PEERS, body, 0, unroll=4)


def row_block(received, n):
    return received[n // 2, n % 2 * PAIRS : (n % 2 + 1) * PAIRS, :]


def row_coefficients(coef_own):
    mine = coef_own[...].astype(F32)
    return jnp.concatenate([mine, mine], axis=0).astype(BF16)


def put_pieces(received, kc, target, at):
    for p in range(8):
        target[at + p // 2, p % 2 * 8 : p % 2 * 8 + 8, :] = received[kc * 8 + p, 2 * PAIRS :, :]


def split_kernel(received, coef_own, mine, up, down, across):
    kc = lax.axis_index("kc")
    for n in range(64):
        block = row_block(received, n)
        for target in (mine, up, down):
            target[n] = block
    for step, target, at in ((1, up, 64), (3, down, 64), (2, across, 0)):
        put_pieces(received, (kc + step) % 4, target, at)
        target[at + 4] = row_coefficients(coef_own)


def collect_kernel(received, left, right, far_coef, collected):
    put_pieces(received, lax.axis_index("kc"), collected, 0)
    for n in range(4):
        collected[4 + n] = left[64 + n]
        collected[8 + n] = right[64 + n]
        collected[12 + n] = far_coef[n]


def spread(row_of, count):
    keep = iota((8, LANES), 1) // PAIRS == iota((8, LANES), 0)
    pieces = []
    for p in range(count):
        for half in range(2):
            pieces.append(jnp.where(keep, jnp.broadcast_to(row_of(p, half), (8, LANES)), 0.0))
    return jnp.concatenate(pieces, axis=0).astype(BF16)


def repeat_matrix():
    same = iota((LANES, LANES), 0) % PAIRS == iota((LANES, LANES), 1) % PAIRS
    return jnp.where(same, 1.0, 0.0).astype(BF16)


def pair_blocks(low_of, high_of, pairs):
    low = iota((PAIRS, LANES), 1) < 64
    for n in range(64):
        first, second = low_of(n), high_of(n)
        pairs[2 * n] = jnp.where(low, first, pltpu.roll(second.astype(F32), 64, 1).astype(BF16))
        pairs[2 * n + 1] = jnp.where(low, pltpu.roll(first.astype(F32), 64, 1).astype(BF16), second)


def turn_points(scalars, first, pairs, turn, picked, turned, v):
    for i in range(64):
        picked[v % 2, i * PAIRS : (i + 1) * PAIRS, :] = pairs[scalars[0, first + 64 * v + i]]
    turned[:, v * 1024 : (v + 1) * 1024] = dot_t(turn, picked[v % 2]).astype(BF16)


def expand_points(turned, cols, result, v):
    for u in range(8 * v, 8 * v + 8):
        at = slice(u * LANES, (u + 1) * LANES)
        result[:, at] = jnp.dot(turned[:, at], cols[u], preferred_element_type=F32).astype(BF16)


def row_copy(result, out, sem, n, step, v):
    row = pl.multiple_of((lax.axis_index("kc") + step) % 4 * 64, 64)
    at = pl.ds(v * 1024, 1024)
    return pltpu.make_async_copy(result.at[pl.ds(n * 64, 64), at], out.at[pl.ds(row, 64), at], sem.at[1 + 4 * n + v])


def diagonal():
    same = iota((LANES, LANES), 0) // PAIRS == iota((LANES, LANES), 1) // PAIRS
    return jnp.where(same, 1.0, 0.0).astype(BF16)


def turn_of(first, second, repeat, diag):
    rows = (first.astype(F32), second.astype(F32))

    def row_of(p, half):
        at = half * POINTS + p % POINTS
        return rows[p // POINTS][at : at + 1]

    return jnp.dot(spread(row_of, 8), repeat, preferred_element_type=F32).astype(BF16) * diag


def turn_kernel(near, mine, coef_own, left, turned, pairs, picked, scalars, sem):
    fetch = index_copy(near, scalars, sem)
    fetch.start()
    kc = lax.axis_index("kc")
    turn = turn_of(coef_own[...], left[68], repeat_matrix(), diagonal())
    pair_blocks(lambda n: mine[n], lambda n: left[n], pairs)
    fetch.wait()
    for v in range(4):
        turn_points(scalars, 256 * kc, pairs, turn, picked, turned, v)


def middle_kernel(
    coef_half, coef_other, right, far_coef, turned, out, cols, turn_far, pieces, diag, result, sem
):
    kc = lax.axis_index("kc")
    repeat = repeat_matrix()
    diag[...] = diagonal()
    turn_far[...] = turn_of(right[68], far_coef[4], repeat, diag[...])
    core = lax.axis_index("kf_2")
    for n, step in enumerate((0, 3, 1, 2)):
        for p in range(8):
            for owner, source in ((core, coef_half), (1 - core, coef_other)):
                piece = source[4 * n + p // 2, p % 2 * 8 : p % 2 * 8 + 8, :].astype(F32)
                pieces[(kc + step) % 4, p, pl.ds(pl.multiple_of(owner * 8, 8), 8), :] = piece

    def build(v):
        for s in range(8):
            p_index, h, par = 2 * v + s // 4, s // 2 % 2, s % 2

            def row_of(p, half):
                r = h * 8 + half * POINTS + p % POINTS
                return pieces[par * 2 + p // POINTS, p_index, r : r + 1, :]

            cols[8 * v + s] = dot_t(repeat, spread(row_of, 8)).astype(BF16) * diag[...]

    for v in range(5):
        if v < 4:
            build(v)
        if v > 0:
            expand_points(turned, cols, result, v - 1)
            for n, step in enumerate((0, 3)):
                row_copy(result, out, sem, n, step, v - 1).start()
    for v in range(4):
        for n, step in enumerate((0, 3)):
            row_copy(result, out, sem, n, step, v).wait()


def last_kernel(near, right, far, cols, turn_far, partial, out, pairs, picked, turned, result, scalars, sem):
    fetch = index_copy(near, scalars, sem)
    fetch.start()
    kc = lax.axis_index("kc")
    pair_blocks(lambda n: right[n], lambda n: far[n], pairs)
    turn = turn_far[...]
    fetch.wait()
    for v in range(5):
        if v < 4:
            turn_points(scalars, 256 * kc, pairs, turn, picked, turned, v)
        if v > 0:
            expand_points(turned, cols, result, v - 1)
            for n, step in enumerate((1, 2)):
                row_copy(result, out, sem, n, step, v - 1).start()
    for v in range(4):
        for n, step in enumerate((1, 2)):
            row_copy(result, out, sem, n, step, v).wait()


def call(kernel, outs, in_specs, out_specs, scratch, flops, aliases=None):
    return pl.pallas_call(
        kernel,
        out_shape=outs,
        in_specs=in_specs,
        out_specs=out_specs,
        scratch_shapes=scratch,
        input_output_aliases=aliases or {},
        compiler_params=pltpu.CompilerParams(vmem_limit_bytes=8 << 20),
        cost_estimate=pl.CostEstimate(flops=flops, bytes_accessed=flops // 10, transcendentals=0),
    )


def shape(*dims):
    return jax.ShapeDtypeStruct(dims, BF16)


def shift(value, by):
    return lax.ppermute(value, "kc", [(i, (i + by) % 4) for i in range(4)])


def partner(value):
    return lax.ppermute(value, "kf_2", [(0, 1), (1, 0)])


def shards(kernel_coarse, coefficients, nearest):
    other = partner(kernel_coarse)
    rotations = (128, 32, LANES)
    block = (PAIRS, LANES)
    table = jnp.pad(nearest.reshape(1, FINE), ((32, 15), (0, FINE))).astype(F32)
    rows = jnp.pad(coefficients.astype(F32), ((40, 4), (0, 2 * FINE - 2 * LANES)))
    fetched = jnp.pad(kernel_coarse.astype(F32), ((0, 16), (0, 0))) + table + rows
    scalars = [pltpu.SMEM((1, FINE), jnp.int32), pltpu.SemaphoreType.DMA((9,))]
    index = jax.ShapeDtypeStruct((1, FINE), jnp.int32)
    own_copies, near, slots, coef_own = call(
        own_kernel, (shape(*rotations), index, index, shape(8, LANES)), [VMEM], (VMEM,) * 4, [], 1000000
    )(fetched)
    packed = call(
        pack_kernel, shape(PEERS, 40, LANES), [VMEM] * 4, VMEM, [pltpu.VMEM(rotations, BF16)] + scalars, 1000000
    )(slots, own_copies, other, coef_own)
    received = lax.all_to_all(packed, ZY, split_axis=0, concat_axis=0, tiled=True)
    mine, up, down, across = call(
        split_kernel, tuple(shape(n, *block) for n in (64, 69, 69, 5)), [VMEM] * 2, (VMEM,) * 4, [], 100000
    )(received, coef_own)
    left = shift(up, 1)
    right = shift(down, -1)
    far_coef = shift(across, 2)
    far = shift(mine, 2)
    coef_half = call(collect_kernel, shape(16, *block), [VMEM] * 4, VMEM, [], 100000)(received, left, right, far_coef)
    coef_other = partner(coef_half)
    pairs = pltpu.VMEM((128, *block), BF16)
    picked = pltpu.VMEM((2, 1024, LANES), BF16)
    turned = pltpu.VMEM((LANES, 4096), BF16)
    rows_turned = call(
        turn_kernel, shape(LANES, 4096), [VMEM] * 4, VMEM, [pairs, picked] + scalars, 2000000
    )(near, mine, coef_own, left)
    partial, cols, turn_far = call(
        middle_kernel,
        (shape(256, 4096), shape(32, LANES, LANES), shape(LANES, LANES)),
        [VMEM] * 5,
        (ANY, VMEM, VMEM),
        [pltpu.VMEM((4, 8, *block), F32), pltpu.VMEM((LANES, LANES), BF16), turned] + scalars[1:],
        8000000,
    )(coef_half, coef_other, right, far_coef, rows_turned)
    return call(
        last_kernel,
        shape(256, 4096),
        [VMEM] * 5 + [ANY],
        ANY,
        [pairs, picked, turned, turned] + scalars,
        3000000,
        {5: 0},
    )(near, right, far, cols, turn_far, partial)


def solution(mesh):
    split = Mesh(mesh.devices.reshape(8, 4, 2, mesh.shape["kc"]), KF_KC)
    return jax.shard_map(
        shards,
        mesh=split,
        in_specs=(P(KF, None), P(KF_KC, None), P()),
        out_specs=P(KF, "kc"),
        check_vma=False,
    )
```

profile of v0, /device:TPU:1, one launch (start us, length us, event | category | flops | bytes accessed | tf_op | source)
XLA Modules:
  0.0 53.2 jit_solution(12858255911914279081)
XLA Ops:
  0.0 3.2 %collective-permute-start = (bf16[32,2048]{1,0:T(8,128)(2,1)}, bf16[32,2048]{1,0:T(8,128)(2,1)S(1)}, u32[]{:S(2)}, u32[]{:S(2)}) collective-permute-start(bf16[32,2048]{1,0:T(8,128)(2,1)} %param.3), channel_id=1, source_target_pairs={{0,4},{4,0},{1,5},{5,1},{2,6},{6,2},{3,7},{7,3},{8,12},{12,8},{9,1... | collective-permute-start | bytes 393224 | tf_op jit(solution)/shard_map/ppermute | solution.py:260
  3.2 1.0 %convert_add_fusion.fetched = f32[48,2048]{1,0:T(8,128)S(1)} fusion(s32[1,1024]{1,0:T(1,128)} %bitcast.1, bf16[4,256]{1,0:T(4,128)(2,1)} %param.4, bf16[32,2048]{1,0:T(8,128)(2,1)} %param.3), kind=kLoop, calls=%fused_computation | loop fusion | flops 491520 | bytes 530432 | tf_op jit(solution)/shard_map/add | solution.py:269
  4.2 0.3 shard_map.37
  4.5 0.0 collective-permute-done.other
  4.5 1.4 %shard_map.38 = bf16[32,40,128]{2,1,0:T(8,128)(2,1)S(1)} custom-call(s32[1,1024]{1,0:T(1,128)S(1)} %get-tuple-element.17.slots, bf16[128,32,128]{2,1,0:T(8,128)(2,1)S(1)} %get-tuple-element.18.own_copies, bf16[32,2048]{1,0:T(8,128)(2,1)S(1)} %collective-permute-done.other, bf16[8,128]{1,0:T(8,128)(2,1)S(1)} %get-tuple-element.19.coef.coef_own), custom_call_target="tpu_custom_call" | custom-call | flops 1000000 | bytes 100000 | tf_op jit(solution)/shard_map/pallas_call | solution.py:275
  5.9 22.2 %all_to_all.5.received = bf16[32,40,128]{2,1,0:T(8,128)(2,1)S(1)} all-to-all(bf16[32,40,128]{2,1,0:T(8,128)(2,1)S(1)} %shard_map.38), channel_id=1, replica_groups=mesh['kf_0'=8,'kf_1'=4,'kf_2'=2,'kc'=4] {'kf_0','kf_1'}, dimensions={0} | all-to-all | bytes 655360 | tf_op jit(solution)/shard_map/all_to_all | solution.py:278
  28.0 0.1 shard_map.39
  28.1 2.6 %collective-permute-start.1 = (bf16[69,16,128]{2,1,0:T(8,128)(2,1)S(1)}, bf16[69,16,128]{2,1,0:T(8,128)(2,1)S(1)}, u32[]{:S(2)}, u32[]{:S(2)}) collective-permute-start(bf16[69,16,128]{2,1,0:T(8,128)(2,1)S(1)} %get-tuple-element.20), channel_id=1, source_target_pairs={{0,3},{1,0},{2,1},{3,2},{4,7},{5,4},{6,5},{7,6},{8,11},{9,8},{10,9... | collective-permute-start | bytes 847880 | tf_op jit(solution)/shard_map/ppermute | solution.py:256
  30.7 0.0 collective-permute-start.3
  30.7 1.7 %collective-permute-start.2 = (bf16[64,16,128]{2,1,0:T(8,128)(2,1)S(1)}, bf16[64,16,128]{2,1,0:T(8,128)(2,1)S(1)}, u32[]{:S(2)}, u32[]{:S(2)}) collective-permute-start(bf16[64,16,128]{2,1,0:T(8,128)(2,1)S(1)} %get-tuple-element.21.mine), channel_id=1, source_target_pairs={{0,2},{1,3},{2,0},{3,1},{4,6},{5,7},{6,4},{7,5},{8,10},{9,11},{10,... | collective-permute-start | bytes 786440 | tf_op jit(solution)/shard_map/ppermute | solution.py:256
  32.4 1.2 %collective-permute-start.4 = (bf16[5,16,128]{2,1,0:T(8,128)(2,1)S(1)}, bf16[5,16,128]{2,1,0:T(8,128)(2,1)S(1)}, u32[]{:S(2)}, u32[]{:S(2)}) collective-permute-start(bf16[5,16,128]{2,1,0:T(8,128)(2,1)S(1)} %get-tuple-element.23), channel_id=1, source_target_pairs={{0,2},{1,3},{2,0},{3,1},{4,6},{5,7},{6,4},{7,5},{8,10},{9,11},{10,... | collective-permute-start | bytes 61448 | tf_op jit(solution)/shard_map/ppermute | solution.py:256
  33.7 8.8 %collective-permute-done.4.far_coef = bf16[5,16,128]{2,1,0:T(8,128)(2,1)S(1)} collective-permute-done((bf16[5,16,128]{2,1,0:T(8,128)(2,1)S(1)}, bf16[5,16,128]{2,1,0:T(8,128)(2,1)S(1)}, u32[]{:S(2)}, u32[]{:S(2)}) %collective-permute-start.4) | collective-permute-done | bytes 20512 | tf_op jit(solution)/shard_map/ppermute | solution.py:256
  42.4 0.0 collective-permute-done.1.right
  42.4 0.0 collective-permute-done.3.left
  42.5 4.8 %collective-permute-start.5 = (bf16[16,16,128]{2,1,0:T(8,128)(2,1)S(1)}, bf16[16,16,128]{2,1,0:T(8,128)(2,1)S(1)}, u32[]{:S(2)}, u32[]{:S(2)}) collective-permute-start(bf16[16,16,128]{2,1,0:T(8,128)(2,1)S(1)} %shard_map.40.coef_half), channel_id=1, source_target_pairs={{0,4},{4,0},{1,5},{5,1},{2,6},{6,2},{3,7},{7,3},{8,12},{12,8},{9,1... | collective-permute-start | bytes 196616 | tf_op jit(solution)/shard_map/ppermute | solution.py:260
  47.2 1.4 %shard_map.41.turned = bf16[128,4096]{1,0:T(8,128)(2,1)S(1)} custom-call(s32[1,1024]{1,0:T(1,128)S(1)} %get-tuple-element.16.near, bf16[64,16,128]{2,1,0:T(8,128)(2,1)S(1)} %get-tuple-element.21.mine, bf16[8,128]{1,0:T(8,128)(2,1)S(1)} %get-tuple-element.19.coef.coef_own, bf16[69,16,128]{2,1,0:T(8,128)(2,1)S(1)} %collective-permute-done.3.left), custom_call_target="tpu_custom_call" | custom-call | flops 2000000 | bytes 200000 | tf_op jit(solution)/shard_map/pallas_call | solution.py:291
  48.6 0.0 collective-permute-done.5.coef_other
  48.6 2.1 %shard_map.42 = (bf16[256,4096]{1,0:T(8,128)(2,1)}, bf16[32,128,128]{2,1,0:T(8,128)(2,1)S(1)}, bf16[128,128]{1,0:T(8,128)(2,1)S(1)}) custom-call(bf16[16,16,128]{2,1,0:T(8,128)(2,1)S(1)} %shard_map.40.coef_half, bf16[16,16,128]{2,1,0:T(8,128)(2,1)S(1)} %collective-permute-done.5.coef_other, bf16[69,16,128]{2,1,0:T(8,128)(2,1)S(1)} %collective-permute-done.1.right, ...), custom_call_target="tpu_custom_call" | custom-call | flops 8000000 | bytes 800000 | tf_op jit(solution)/shard_map/pallas_call | solution.py:294
  50.7 0.0 collective-permute-done.2.far
  50.7 2.5 %shard_map.43 = bf16[256,4096]{1,0:T(8,128)(2,1)} custom-call(s32[1,1024]{1,0:T(1,128)S(1)} %get-tuple-element.16.near, bf16[69,16,128]{2,1,0:T(8,128)(2,1)S(1)} %collective-permute-done.1.right, bf16[64,16,128]{2,1,0:T(8,128)(2,1)S(1)} %collective-permute-done.2.far, ...), custom_call_target="tpu_custom_call", output_to_operand_aliasing={{}: (5, {})} | custom-call | flops 3000000 | bytes 300000 | tf_op jit(solution)/shard_map/pallas_call | solution.py:302
  (1 shorter events, 0.0 us)
Async XLA Ops:
  0.0 4.5 %collective-permute-start = (bf16[32,2048]{1,0:T(8,128)(2,1)}, bf16[32,2048]{1,0:T(8,128)(2,1)S(1)}, u32[]{:S(2)}, u32[]{:S(2)}) collective-permute-start(bf16[32,2048]{1,0:T(8,128)(2,1)} %param.3), channel_id=1, source_target_pairs={{0,4},{4,0},{1,5},{5,1},{2,6},{6,2},{3,7},{7,3},{8,12},{12,8},{9,1... | collective-permute-start | bytes 393224 | tf_op jit(solution)/shard_map/ppermute | solution.py:260
  28.1 14.3 %collective-permute-start.1 = (bf16[69,16,128]{2,1,0:T(8,128)(2,1)S(1)}, bf16[69,16,128]{2,1,0:T(8,128)(2,1)S(1)}, u32[]{:S(2)}, u32[]{:S(2)}) collective-permute-start(bf16[69,16,128]{2,1,0:T(8,128)(2,1)S(1)} %get-tuple-element.20), channel_id=1, source_target_pairs={{0,3},{1,0},{2,1},{3,2},{4,7},{5,4},{6,5},{7,6},{8,11},{9,8},{10,9... | collective-permute-start | bytes 847880 | tf_op jit(solution)/shard_map/ppermute | solution.py:256
  30.7 11.8 %collective-permute-start.3 = (bf16[69,16,128]{2,1,0:T(8,128)(2,1)S(1)}, bf16[69,16,128]{2,1,0:T(8,128)(2,1)S(1)}, u32[]{:S(2)}, u32[]{:S(2)}) collective-permute-start(bf16[69,16,128]{2,1,0:T(8,128)(2,1)S(1)} %get-tuple-element.22), channel_id=1, source_target_pairs={{0,1},{1,2},{2,3},{3,0},{4,5},{5,6},{6,7},{7,4},{8,9},{9,10},{10,1... | collective-permute-start | bytes 847880 | tf_op jit(solution)/shard_map/ppermute | solution.py:256
  30.7 20.0 %collective-permute-start.2 = (bf16[64,16,128]{2,1,0:T(8,128)(2,1)S(1)}, bf16[64,16,128]{2,1,0:T(8,128)(2,1)S(1)}, u32[]{:S(2)}, u32[]{:S(2)}) collective-permute-start(bf16[64,16,128]{2,1,0:T(8,128)(2,1)S(1)} %get-tuple-element.21.mine), channel_id=1, source_target_pairs={{0,2},{1,3},{2,0},{3,1},{4,6},{5,7},{6,4},{7,5},{8,10},{9,11},{10,... | collective-permute-start | bytes 786440 | tf_op jit(solution)/shard_map/ppermute | solution.py:256
  32.4 10.0 %collective-permute-start.4 = (bf16[5,16,128]{2,1,0:T(8,128)(2,1)S(1)}, bf16[5,16,128]{2,1,0:T(8,128)(2,1)S(1)}, u32[]{:S(2)}, u32[]{:S(2)}) collective-permute-start(bf16[5,16,128]{2,1,0:T(8,128)(2,1)S(1)} %get-tuple-element.23), channel_id=1, source_target_pairs={{0,2},{1,3},{2,0},{3,1},{4,6},{5,7},{6,4},{7,5},{8,10},{9,11},{10,... | collective-permute-start | bytes 61448 | tf_op jit(solution)/shard_map/ppermute | solution.py:256
  42.5 6.1 %collective-permute-start.5 = (bf16[16,16,128]{2,1,0:T(8,128)(2,1)S(1)}, bf16[16,16,128]{2,1,0:T(8,128)(2,1)S(1)}, u32[]{:S(2)}, u32[]{:S(2)}) collective-permute-start(bf16[16,16,128]{2,1,0:T(8,128)(2,1)S(1)} %shard_map.40.coef_half), channel_id=1, source_target_pairs={{0,4},{4,0},{1,5},{5,1},{2,6},{6,2},{3,7},{7,3},{8,12},{12,8},{9,1... | collective-permute-start | bytes 196616 | tf_op jit(solution)/shard_map/ppermute | solution.py:260
where the time goes:
time: 53.3 us; the launch traced here: 53.2 us
  blocking collectives  22.2 us (42%)
  starting transfers between devices  13.5 us (25%)
  waiting for transfers between devices  8.79 us (16%)
  Pallas kernels  7.74 us (15%)
  other arithmetic  0.96 us (2%)
    all_to_all x1, blocking collectives, shards(): lax.all_to_all(packed, ZY, split_axis=0, concat_axis=0, tiled=True)  22.2 us
    ppermute x4, waiting for transfers between devices, shift(): return lax.ppermute(value, 'kc', [(i, (i + by) % 4) for i in range(4)])  8.78 us
    ppermute x2, starting transfers between devices, partner(): return lax.ppermute(value, 'kf_2', [(0, 1), (1, 0)])  7.95 us
    ppermute x4, starting transfers between devices, shift(): return lax.ppermute(value, 'kc', [(i, (i + by) % 4) for i in range(4)])  5.53 us
    pallas_call x1, Pallas kernels, shards(): call(last_kernel, shape(256, 4096), [VMEM] * 5 + [ANY], ANY, [pairs, pick...  2.51 us
    pallas_call x1, Pallas kernels, shards(): call(middle_kernel, (shape(256, 4096), shape(32, LANES, LANES), shape(LAN...  2.06 us
    pallas_call x1, Pallas kernels, shards(): call(pack_kernel, shape(PEERS, 40, LANES), [VMEM] * 4, VMEM, [pltpu.VMEM(...  1.38 us
    pallas_call x1, Pallas kernels, shards(): call(turn_kernel, shape(LANES, 4096), [VMEM] * 4, VMEM, [pairs, picked] +...  1.37 us
  transfers between devices with their start and end apart: 6, of which 1 were waited for; matrix products, arithmetic and copies ran while one was open for 2% of the time, Pallas kernels for 7%

commit v1 on v0

--- a/solution.py
+++ b/solution.py
@@ -54,13 +54,16 @@
     return pltpu.make_async_copy(near, scalars, sem.at[0])
 
 
-def pack_kernel(slots, own_copies, other, coef, out, other_copies, scalars, sem):
+def pack_kernel(slots, own_copies, other, coef_own, coef_other, out, other_copies, scalars, sem):
     fetch = index_copy(slots, scalars, sem)
     fetch.start()
     kc = lax.axis_index("kc")
     core = lax.axis_index("kf_2")
     turn_rows(other, other_copies)
     copies = (own_copies, other_copies)
+    a = coef_own[...].astype(F32)
+    o = halves_stacked(coef_other[...].astype(F32))
+    coef = jnp.concatenate([jnp.where(core == 0, a, o), jnp.where(core == 0, o, a)], axis=0).astype(BF16)
     fetch.wait()
     group = iota((PAIRS, LANES), 1) // PAIRS
     base = 16 * core + 4 * kc
@@ -75,7 +78,7 @@
                     tiles[n] = piece if tiles[n] is None else jnp.where(group == lo * POINTS + j, piece, tiles[n])
         out[d, pl.ds(pl.multiple_of(core * PAIRS, PAIRS), PAIRS), :] = tiles[0]
         out[d, pl.ds(pl.multiple_of((1 - core) * PAIRS, PAIRS), PAIRS), :] = tiles[1]
-        out[d, 2 * PAIRS :, :] = coef[...]
+        out[d, 2 * PAIRS :, :] = coef
         return carry
 
     lax.fori_loop(0, PEERS, body, 0, unroll=4)
@@ -88,11 +91,6 @@
 def row_coefficients(coef_own):
     mine = coef_own[...].astype(F32)
     return jnp.concatenate([mine, mine], axis=0).astype(BF16)
-
-
-def put_pieces(received, kc, target, at):
-    for p in range(8):
-        target[at + p // 2, p % 2 * 8 : p % 2 * 8 + 8, :] = received[kc * 8 + p, 2 * PAIRS :, :]
 
 
 def split_kernel(received, coef_own, mine, up, down, across):
@@ -102,16 +100,10 @@
         for target in (mine, up, down):
             target[n] = block
     for step, target, at in ((1, up, 64), (3, down, 64), (2, across, 0)):
-        put_pieces(received, (kc + step) % 4, target, at)
-        target[at + 4] = row_coefficients(coef_own)
-
-
-def collect_kernel(received, left, right, far_coef, collected):
-    put_pieces(received, lax.axis_index("kc"), collected, 0)
-    for n in range(4):
-        collected[4 + n] = left[64 + n]
-        collected[8 + n] = right[64 + n]
-        collected[12 + n] = far_coef[n]
+        first = (kc + step) % 4 * 8
+        for p in range(8):
+            target[at + p] = received[first + p, 2 * PAIRS :, :]
+        target[at + 8] = row_coefficients(coef_own)
 
 
 def spread(row_of, count):
@@ -169,30 +161,23 @@
     return jnp.dot(spread(row_of, 8), repeat, preferred_element_type=F32).astype(BF16) * diag
 
 
-def turn_kernel(near, mine, coef_own, left, turned, pairs, picked, scalars, sem):
+def middle_kernel(
+    near, received, mine, coef_own, left, right, far_coef, out, cols, turn_far,
+    pieces, pairs, diag, picked, turned, result, scalars, sem
+):
     fetch = index_copy(near, scalars, sem)
     fetch.start()
     kc = lax.axis_index("kc")
-    turn = turn_of(coef_own[...], left[68], repeat_matrix(), diagonal())
-    pair_blocks(lambda n: mine[n], lambda n: left[n], pairs)
-    fetch.wait()
-    for v in range(4):
-        turn_points(scalars, 256 * kc, pairs, turn, picked, turned, v)
-
-
-def middle_kernel(
-    coef_half, coef_other, right, far_coef, turned, out, cols, turn_far, pieces, diag, result, sem
-):
-    kc = lax.axis_index("kc")
     repeat = repeat_matrix()
     diag[...] = diagonal()
-    turn_far[...] = turn_of(right[68], far_coef[4], repeat, diag[...])
-    core = lax.axis_index("kf_2")
-    for n, step in enumerate((0, 3, 1, 2)):
-        for p in range(8):
-            for owner, source in ((core, coef_half), (1 - core, coef_other)):
-                piece = source[4 * n + p // 2, p % 2 * 8 : p % 2 * 8 + 8, :].astype(F32)
-                pieces[(kc + step) % 4, p, pl.ds(pl.multiple_of(owner * 8, 8), 8), :] = piece
+    turn = turn_of(coef_own[...], left[72], repeat, diag[...])
+    turn_far[...] = turn_of(right[72], far_coef[8], repeat, diag[...])
+    for p in range(8):
+        pieces[kc, p] = received[kc * 8 + p, 2 * PAIRS :, :].astype(F32)
+        pieces[(kc + 3) % 4, p] = left[64 + p].astype(F32)
+        pieces[(kc + 1) % 4, p] = right[64 + p].astype(F32)
+        pieces[(kc + 2) % 4, p] = far_coef[p].astype(F32)
+    pair_blocks(lambda n: mine[n], lambda n: left[n], pairs)
 
     def build(v):
         for s in range(8):
@@ -204,9 +189,13 @@
 
             cols[8 * v + s] = dot_t(repeat, spread(row_of, 8)).astype(BF16) * diag[...]
 
+    build(0)
+    fetch.wait()
     for v in range(5):
         if v < 4:
-            build(v)
+            turn_points(scalars, 256 * kc, pairs, turn, picked, turned, v)
+            if v > 0:
+                build(v)
         if v > 0:
             expand_points(turned, cols, result, v - 1)
             for n, step in enumerate((0, 3)):
@@ -262,6 +251,7 @@
 
 def shards(kernel_coarse, coefficients, nearest):
     other = partner(kernel_coarse)
+    coef_other = partner(coefficients)
     rotations = (128, 32, LANES)
     block = (PAIRS, LANES)
     table = jnp.pad(nearest.reshape(1, FINE), ((32, 15), (0, FINE))).astype(F32)
@@ -273,32 +263,27 @@
         own_kernel, (shape(*rotations), index, index, shape(8, LANES)), [VMEM], (VMEM,) * 4, [], 1000000
     )(fetched)
     packed = call(
-        pack_kernel, shape(PEERS, 40, LANES), [VMEM] * 4, VMEM, [pltpu.VMEM(rotations, BF16)] + scalars, 1000000
-    )(slots, own_copies, other, coef_own)
+        pack_kernel, shape(PEERS, 48, LANES), [VMEM] * 5, VMEM, [pltpu.VMEM(rotations, BF16)] + scalars, 1000000
+    )(slots, own_copies, other, coef_own, coef_other)
     received = lax.all_to_all(packed, ZY, split_axis=0, concat_axis=0, tiled=True)
     mine, up, down, across = call(
-        split_kernel, tuple(shape(n, *block) for n in (64, 69, 69, 5)), [VMEM] * 2, (VMEM,) * 4, [], 100000
+        split_kernel, tuple(shape(n, *block) for n in (64, 73, 73, 9)), [VMEM] * 2, (VMEM,) * 4, [], 100000
     )(received, coef_own)
     left = shift(up, 1)
     right = shift(down, -1)
     far_coef = shift(across, 2)
     far = shift(mine, 2)
-    coef_half = call(collect_kernel, shape(16, *block), [VMEM] * 4, VMEM, [], 100000)(received, left, right, far_coef)
-    coef_other = partner(coef_half)
     pairs = pltpu.VMEM((128, *block), BF16)
     picked = pltpu.VMEM((2, 1024, LANES), BF16)
     turned = pltpu.VMEM((LANES, 4096), BF16)
-    rows_turned = call(
-        turn_kernel, shape(LANES, 4096), [VMEM] * 4, VMEM, [pairs, picked] + scalars, 2000000
-    )(near, mine, coef_own, left)
     partial, cols, turn_far = call(
         middle_kernel,
         (shape(256, 4096), shape(32, LANES, LANES), shape(LANES, LANES)),
-        [VMEM] * 5,
+        [VMEM] * 7,
         (ANY, VMEM, VMEM),
-        [pltpu.VMEM((4, 8, *block), F32), pltpu.VMEM((LANES, LANES), BF16), turned] + scalars[1:],
+        [pltpu.VMEM((4, 8, *block), F32), pairs, pltpu.VMEM((LANES, LANES), BF16), picked, turned, turned] + scalars,
         8000000,
-    )(coef_half, coef_other, right, far_coef, rows_turned)
+    )(near, received, mine, coef_own, left, right, far_coef)
     return call(
         last_kernel,
         shape(256, 4096),

time: 53.3 us -> 53 us (level)
  the two profiles are of different devices: /device:TPU:1 before, /device:TPU:8 now
where the time goes in v1:
time: 53 us; the launch traced here: 52.9 us
  blocking collectives  25.9 us (49%)
  waiting for transfers between devices  11.7 us (22%)
  Pallas kernels  7.32 us (14%)
  starting transfers between devices  6.88 us (13%)
  other arithmetic  0.96 us (2%)
    all_to_all x1, blocking collectives, shards(): lax.all_to_all(packed, ZY, split_axis=0, concat_axis=0, tiled=True)  25.9 us
    ppermute x4, waiting for transfers between devices, shift(): return lax.ppermute(value, 'kc', [(i, (i + by) % 4) for i in range(4)])  11.7 us
    ppermute x4, starting transfers between devices, shift(): return lax.ppermute(value, 'kc', [(i, (i + by) % 4) for i in range(4)])  6.37 us
    pallas_call x1, Pallas kernels, shards(): call(middle_kernel, (shape(256, 4096), shape(32, LANES, LANES), shape(LAN...  3.02 us
    pallas_call x1, Pallas kernels, shards(): call(last_kernel, shape(256, 4096), [VMEM] * 5 + [ANY], ANY, [pairs, pick...  2.52 us
    pallas_call x1, Pallas kernels, shards(): call(pack_kernel, shape(PEERS, 48, LANES), [VMEM] * 5, VMEM, [pltpu.VMEM(...  1.36 us
  transfers between devices with their start and end apart: 6, of which 2 were waited for; matrix products, arithmetic and copies ran while one was open for 2% of the time, Pallas kernels for 6%

profile of v1, /device:TPU:8, one launch (start us, length us, event | category | flops | bytes accessed | tf_op | source)
XLA Modules:
  0.0 52.9 jit_solution(13017280798371829504)
XLA Ops:
  0.0 0.0 collective-permute-start.1
  0.0 0.5 collective-permute-start
  0.5 1.0 %convert_add_fusion.fetched = f32[48,2048]{1,0:T(8,128)S(1)} fusion(s32[1,1024]{1,0:T(1,128)} %bitcast.1, bf16[4,256]{1,0:T(4,128)(2,1)} %param.4, bf16[32,2048]{1,0:T(8,128)(2,1)} %param.3), kind=kLoop, calls=%fused_computation | loop fusion | flops 491520 | bytes 530432 | tf_op jit(solution)/shard_map/add | solution.py:259
  1.5 0.3 shard_map.37
  1.8 0.0 collective-permute-done.1.coef_other
  1.8 0.0 collective-permute-done.other
  1.8 1.4 %shard_map.38 = bf16[32,48,128]{2,1,0:T(8,128)(2,1)S(1)} custom-call(s32[1,1024]{1,0:T(1,128)S(1)} %get-tuple-element.17.slots, bf16[128,32,128]{2,1,0:T(8,128)(2,1)S(1)} %get-tuple-element.18.own_copies, bf16[32,2048]{1,0:T(8,128)(2,1)S(1)} %collective-permute-done.other, bf16[8,128]{1,0:T(8,128)(2,1)S(1)} %get-tuple-element.19.coef_own, ...), custom_call_target="tpu_custom_call" | custom-call | flops 1000000 | bytes 100000 | tf_op jit(solution)/shard_map/pallas_call | solution.py:265
  3.2 25.9 %all_to_all.5.received = bf16[32,48,128]{2,1,0:T(8,128)(2,1)S(1)} all-to-all(bf16[32,48,128]{2,1,0:T(8,128)(2,1)S(1)} %shard_map.38), channel_id=1, replica_groups=mesh['kf_0'=8,'kf_1'=4,'kf_2'=2,'kc'=4] {'kf_0','kf_1'}, dimensions={0} | all-to-all | bytes 786432 | tf_op jit(solution)/shard_map/all_to_all | solution.py:268
  29.1 0.1 shard_map.39
  29.2 2.8 %collective-permute-start.2 = (bf16[73,16,128]{2,1,0:T(8,128)(2,1)S(1)}, bf16[73,16,128]{2,1,0:T(8,128)(2,1)S(1)}, u32[]{:S(2)}, u32[]{:S(2)}) collective-permute-start(bf16[73,16,128]{2,1,0:T(8,128)(2,1)S(1)} %get-tuple-element.20), channel_id=1, source_target_pairs={{0,3},{1,0},{2,1},{3,2},{4,7},{5,4},{6,5},{7,6},{8,11},{9,8},{10,9... | collective-permute-start | bytes 897032 | tf_op jit(solution)/shard_map/ppermute | solution.py:245
  32.1 0.0 collective-permute-start.4
  32.1 2.3 %collective-permute-start.3 = (bf16[64,16,128]{2,1,0:T(8,128)(2,1)S(1)}, bf16[64,16,128]{2,1,0:T(8,128)(2,1)S(1)}, u32[]{:S(2)}, u32[]{:S(2)}) collective-permute-start(bf16[64,16,128]{2,1,0:T(8,128)(2,1)S(1)} %get-tuple-element.21.mine), channel_id=1, source_target_pairs={{0,2},{1,3},{2,0},{3,1},{4,6},{5,7},{6,4},{7,5},{8,10},{9,11},{10,... | collective-permute-start | bytes 786440 | tf_op jit(solution)/shard_map/ppermute | solution.py:245
  34.4 1.2 %collective-permute-start.5 = (bf16[9,16,128]{2,1,0:T(8,128)(2,1)S(1)}, bf16[9,16,128]{2,1,0:T(8,128)(2,1)S(1)}, u32[]{:S(2)}, u32[]{:S(2)}) collective-permute-start(bf16[9,16,128]{2,1,0:T(8,128)(2,1)S(1)} %get-tuple-element.23), channel_id=1, source_target_pairs={{0,2},{1,3},{2,0},{3,1},{4,6},{5,7},{6,4},{7,5},{8,10},{9,11},{10,... | collective-permute-start | bytes 110600 | tf_op jit(solution)/shard_map/ppermute | solution.py:245
  35.6 10.9 %collective-permute-done.5.far_coef = bf16[9,16,128]{2,1,0:T(8,128)(2,1)S(1)} collective-permute-done((bf16[9,16,128]{2,1,0:T(8,128)(2,1)S(1)}, bf16[9,16,128]{2,1,0:T(8,128)(2,1)S(1)}, u32[]{:S(2)}, u32[]{:S(2)}) %collective-permute-start.5) | collective-permute-done | bytes 36896 | tf_op jit(solution)/shard_map/ppermute | solution.py:245
  46.5 0.0 collective-permute-done.2.right
  46.5 0.8 %collective-permute-done.4.left = bf16[73,16,128]{2,1,0:T(8,128)(2,1)S(1)} collective-permute-done((bf16[73,16,128]{2,1,0:T(8,128)(2,1)S(1)}, bf16[73,16,128]{2,1,0:T(8,128)(2,1)S(1)}, u32[]{:S(2)}, u32[]{:S(2)}) %collective-permute-start.4) | collective-permute-done | bytes 299040 | tf_op jit(solution)/shard_map/ppermute | solution.py:245
  47.3 3.0 %shard_map.40 = (bf16[256,4096]{1,0:T(8,128)(2,1)}, bf16[32,128,128]{2,1,0:T(8,128)(2,1)S(1)}, bf16[128,128]{1,0:T(8,128)(2,1)S(1)}) custom-call(s32[1,1024]{1,0:T(1,128)S(1)} %get-tuple-element.16.near, bf16[32,48,128]{2,1,0:T(8,128)(2,1)S(1)} %all_to_all.5.received, bf16[64,16,128]{2,1,0:T(8,128)(2,1)S(1)} %get-tuple-element.21.mine, ...), custom_call_target="tpu_custom_call" | custom-call | flops 8000000 | bytes 800000 | tf_op jit(solution)/shard_map/pallas_call | solution.py:279
  50.4 0.0 collective-permute-done.3.far
  50.4 2.5 %shard_map.41 = bf16[256,4096]{1,0:T(8,128)(2,1)} custom-call(s32[1,1024]{1,0:T(1,128)S(1)} %get-tuple-element.16.near, bf16[73,16,128]{2,1,0:T(8,128)(2,1)S(1)} %collective-permute-done.2.right, bf16[64,16,128]{2,1,0:T(8,128)(2,1)S(1)} %collective-permute-done.3.far, ...), custom_call_target="tpu_custom_call", output_to_operand_aliasing={{}: (5, {})} | custom-call | flops 3000000 | bytes 300000 | tf_op jit(solution)/shard_map/pallas_call | solution.py:287
Async XLA Ops:
  0.0 1.8 %collective-permute-start.1 = (bf16[4,256]{1,0:T(4,128)(2,1)}, bf16[4,256]{1,0:T(4,128)(2,1)S(1)}, u32[]{:S(2)}, u32[]{:S(2)}) collective-permute-start(bf16[4,256]{1,0:T(4,128)(2,1)} %param.4), channel_id=1, source_target_pairs={{0,4},{4,0},{1,5},{5,1},{2,6},{6,2},{3,7},{7,3},{8,12},{12,8},{9,1... | collective-permute-start | bytes 6152 | tf_op jit(solution)/shard_map/ppermute | solution.py:249
  0.0 1.8 %collective-permute-start = (bf16[32,2048]{1,0:T(8,128)(2,1)}, bf16[32,2048]{1,0:T(8,128)(2,1)S(1)}, u32[]{:S(2)}, u32[]{:S(2)}) collective-permute-start(bf16[32,2048]{1,0:T(8,128)(2,1)} %param.3), channel_id=1, source_target_pairs={{0,4},{4,0},{1,5},{5,1},{2,6},{6,2},{3,7},{7,3},{8,12},{12,8},{9,1... | collective-permute-start | bytes 393224 | tf_op jit(solution)/shard_map/ppermute | solution.py:249
  29.2 17.3 %collective-permute-start.2 = (bf16[73,16,128]{2,1,0:T(8,128)(2,1)S(1)}, bf16[73,16,128]{2,1,0:T(8,128)(2,1)S(1)}, u32[]{:S(2)}, u32[]{:S(2)}) collective-permute-start(bf16[73,16,128]{2,1,0:T(8,128)(2,1)S(1)} %get-tuple-element.20), channel_id=1, source_target_pairs={{0,3},{1,0},{2,1},{3,2},{4,7},{5,4},{6,5},{7,6},{8,11},{9,8},{10,9... | collective-permute-start | bytes 897032 | tf_op jit(solution)/shard_map/ppermute | solution.py:245
  32.1 15.3 %collective-permute-start.4 = (bf16[73,16,128]{2,1,0:T(8,128)(2,1)S(1)}, bf16[73,16,128]{2,1,0:T(8,128)(2,1)S(1)}, u32[]{:S(2)}, u32[]{:S(2)}) collective-permute-start(bf16[73,16,128]{2,1,0:T(8,128)(2,1)S(1)} %get-tuple-element.22), channel_id=1, source_target_pairs={{0,1},{1,2},{2,3},{3,0},{4,5},{5,6},{6,7},{7,4},{8,9},{9,10},{10,1... | collective-permute-start | bytes 897032 | tf_op jit(solution)/shard_map/ppermute | solution.py:245
  32.1 18.3 %collective-permute-start.3 = (bf16[64,16,128]{2,1,0:T(8,128)(2,1)S(1)}, bf16[64,16,128]{2,1,0:T(8,128)(2,1)S(1)}, u32[]{:S(2)}, u32[]{:S(2)}) collective-permute-start(bf16[64,16,128]{2,1,0:T(8,128)(2,1)S(1)} %get-tuple-element.21.mine), channel_id=1, source_target_pairs={{0,2},{1,3},{2,0},{3,1},{4,6},{5,7},{6,4},{7,5},{8,10},{9,11},{10,... | collective-permute-start | bytes 786440 | tf_op jit(solution)/shard_map/ppermute | solution.py:245
  34.4 12.1 %collective-permute-start.5 = (bf16[9,16,128]{2,1,0:T(8,128)(2,1)S(1)}, bf16[9,16,128]{2,1,0:T(8,128)(2,1)S(1)}, u32[]{:S(2)}, u32[]{:S(2)}) collective-permute-start(bf16[9,16,128]{2,1,0:T(8,128)(2,1)S(1)} %get-tuple-element.23), channel_id=1, source_target_pairs={{0,2},{1,3},{2,0},{3,1},{4,6},{5,7},{6,4},{7,5},{8,10},{9,11},{10,... | collective-permute-start | bytes 110600 | tf_op jit(solution)/shard_map/ppermute | solution.py:245
